TPU v7x, 32 devices: a whole 2x2x4 slice. The times are simulated.
32 devices in a mesh: cat: 2 (over x), lat: 4 (over y, core), lon: 4 (over z).
Axes of the slice: x: 2, y: 2, z: 4, core: 2. Of those that a mesh axis runs over, the one named last changes fastest.
Arguments:
- thickness: bfloat16 [40, 1024, 2560], P('cat', 'lat', 'lon'), may hold values from 0.099609375 to 4
- area: bfloat16 [40, 1024, 2560], P('cat', 'lat', 'lon'), may hold values from 0.0049743652 to 0.049804688
- ridge_weight: float32 [40], P('cat'), may hold values from 0.2 to 2
- cat_top: int32 [1024, 2560], P('lat', 'lon'), may hold values from 1 to 40
- land_mask: int32 [1024, 2560], P('lat', 'lon'), may hold values 0 or 1
- velocity_u: float32 [1024, 2560], P('lat', 'lon'), may hold values from -1.8 to 1.8
- velocity_v: float32 [1024, 2560], P('lat', 'lon'), may hold values from -1.8 to 1.8
- stress_div: float32 [1024, 2560], P('lat', 'lon'), may hold values from -3 to 3
- stress_ten: float32 [1024, 2560], P('lat', 'lon'), may hold values from -3 to 3
- stress_shear: float32 [1024, 2560], P('lat', 'lon'), may hold values from -3 to 3
- wind_x: float32 [1024, 2560], P('lat', 'lon'), may hold values from -6 to 6
- wind_y: float32 [1024, 2560], P('lat', 'lon'), may hold values from -6 to 6
- water_drag: float32 [1024, 2560], P('lat', 'lon'), may hold values from 0.2 to 2
Outputs:
- new_u: float32 [1024, 2560], P('lat', 'lon')
- new_v: float32 [1024, 2560], P('lat', 'lon')
- new_div: float32 [1024, 2560], P('lat', 'lon')
- new_ten: float32 [1024, 2560], P('lat', 'lon')
- new_shear: float32 [1024, 2560], P('lat', 'lon')
Inputs may be any that keep to these rules, and one draw needn't show every extreme that they name: Categories with index cat_top or above are absent from a cell.
All inputs are finite; a program needn't handle non-finite values. No bound on the sum of `land_mask` on one device may be relied on, other than what follows from the above.
Results may differ from a plain program's by a relative error of at most 0.0003.
Values sent between devices are 32-bit elements; how exact they have to be, the bound alone decides.
No kernel may reach another device: no remote copies, remote signals or barrier semaphores. Data moves between devices by JAX's collectives and lax.ppermute only.
A program may use at most 128 MiB of HBM per device.

v0:
```python
import jax
import jax.numpy as jnp
from jax import lax
from jax.sharding import PartitionSpec as P

SUB = 4


ELASTIC = 2.0
ECC_SQUARED = 4.0
DELTA_FLOOR = 0.05
CORIOLIS = 0.5


def extended(cells, sides, width, closed):
    for axis, dim in sides:
        count = lax.axis_size(axis)
        ends = count if closed else count - 1
        head = lax.slice_in_dim(cells, 0, width, axis=dim)
        tail = lax.slice_in_dim(cells, cells.shape[dim] - width, cells.shape[dim], axis=dim)
        cells = jnp.concatenate(
            [
                lax.ppermute(tail, axis, [(i, (i + 1) % count) for i in range(ends)]),
                cells,
                lax.ppermute(head, axis, [((i + 1) % count, i) for i in range(ends)]),
            ],
            axis=dim,
        )
    return cells


def slopes(along, across):
    return (
        0.5 * (along[:, :, 2:] - along[:, :, :-2]),
        0.5 * (across[:, 2:, :] - across[:, :-2, :]),
    )


def local_pad(along_stack, across_stack):
    along = jnp.pad(along_stack, ((0, 0), (0, 0), (1, 1)))
    across = jnp.pad(across_stack, ((0, 0), (1, 1), (0, 0)))
    return (along, across)


def subcycle(velocity, stresses, statics, velocity_pad, stress_pad):
    strength, mass, concentration, drag, push_x, push_y, wet = statics
    along, across = velocity_pad(velocity, velocity)
    ddx, ddy = slopes(along, across)
    divergence = ddx[0] + ddy[1]
    tension = ddx[0] - ddy[1]
    shearing = ddy[0] + ddx[1]
    delta = jnp.sqrt(
        divergence * divergence
        + (tension * tension + shearing * shearing) / ECC_SQUARED
        + DELTA_FLOOR * DELTA_FLOOR
    )
    relax = 1.0 / (1.0 + ELASTIC)
    viscous = ELASTIC * strength / delta
    first = wet * (stresses[0] + viscous * (divergence - delta)) * relax
    second = wet * (stresses[1] + viscous * tension / ECC_SQUARED) * relax
    cross = wet * (stresses[2] + viscous * shearing / ECC_SQUARED) * relax
    normal_x = 0.5 * (first + second)
    normal_y = 0.5 * (first - second)
    along_s, across_s = stress_pad(jnp.stack([normal_x, cross]), jnp.stack([cross, normal_y]))
    sdx, sdy = slopes(along_s, across_s)
    force_x = sdx[0] + sdy[0]
    force_y = sdx[1] + sdy[1]
    denom = mass + drag + 1.0 - wet
    speed_u = (
        wet
        * (mass * velocity[0] + force_x + concentration * push_x + CORIOLIS * mass * velocity[1])
        / denom
    )
    speed_v = (
        wet
        * (mass * velocity[1] + force_y + concentration * push_y - CORIOLIS * mass * velocity[0])
        / denom
    )
    return (jnp.stack([speed_u, speed_v]), jnp.stack([first, second, cross]))


def shards(
    thickness,
    area,
    ridge_weight,
    cat_top,
    land_mask,
    velocity_u,
    velocity_v,
    stress_div,
    stress_ten,
    stress_shear,
    wind_x,
    wind_y,
    water_drag,
):
    local_cats = thickness.shape[0]
    level = lax.axis_index("cat") * local_cats + lax.broadcasted_iota(jnp.int32, thickness.shape, 0)
    present = (level < cat_top[None]).astype(jnp.float32)
    height = thickness.astype(jnp.float32)
    cover = area.astype(jnp.float32) * present
    weighted = ridge_weight[:, None, None] * cover * height * height
    strength, mass, concentration = lax.psum(
        (jnp.sum(weighted, axis=0), jnp.sum(cover * height, axis=0), jnp.sum(cover, axis=0)), "cat"
    )
    wet = land_mask.astype(jnp.float32)
    margin = 2 * SUB
    bundle = jnp.stack(
        [
            strength,
            mass,
            concentration,
            water_drag,
            wind_x,
            wind_y,
            wet,
            velocity_u,
            velocity_v,
            stress_div,
            stress_ten,
            stress_shear,
        ]
    )
    widened = extended(bundle, (("lon", 2),), margin, True)
    padded = extended(widened, (("lat", 1),), margin, False)
    statics = tuple((padded[index] for index in range(7)))
    velocity = padded[7:9]
    stresses = padded[9:12]
    for step in range(SUB):
        velocity, stresses = subcycle(velocity, stresses, statics, local_pad, local_pad)
    rows = velocity.shape[1] - margin
    cols = velocity.shape[2] - margin
    velocity = velocity[:, margin:rows, margin:cols]
    stresses = stresses[:, margin:rows, margin:cols]
    return (velocity[0], velocity[1], stresses[0], stresses[1], stresses[2])


def solution(mesh):
    return jax.shard_map(
        shards,
        mesh=mesh,
        in_specs=(
            P("cat", "lat", "lon"),
            P("cat", "lat", "lon"),
            P("cat"),
            P("lat", "lon"),
            P("lat", "lon"),
            P("lat", "lon"),
            P("lat", "lon"),
            P("lat", "lon"),
            P("lat", "lon"),
            P("lat", "lon"),
            P("lat", "lon"),
            P("lat", "lon"),
            P("lat", "lon"),
        ),
        out_specs=(
            P("lat", "lon"),
            P("lat", "lon"),
            P("lat", "lon"),
            P("lat", "lon"),
            P("lat", "lon"),
        ),
        check_vma=False,
    )
```

profile of v0, /device:TPU:1, one launch (start us, length us, event | category | flops | bytes accessed | tf_op | source)
XLA Modules:
  0.0 152.7 jit_solution(10961664660529904791)
XLA Ops:
  7.2 9.6 %fusion = (f32[256,640]{1,0:T(8,128)}, f32[256,640]{1,0:T(8,128)}, f32[256,640]{1,0:T(8,128)}) fusion(bf16[20,256,640]{2,1,0:T(8,128)(2,1)} %param.13, bf16[20,256,640]{2,1,0:T(8,128)(2,1)} %param.14, s32[256,640]{1,0:T(8,128)} %param.16, s32[20]{0:T(128)S(1)} %iota_add_fusion, f32[20]{0:T(128)} %param.15), kind=kLoop, calls=%fused_computation.2 | loop fusion | flops 35553280 | bytes 15728800 | tf_op jit(solution)/shard_map/reduce_sum | solution.py:104
  16.9 62.2 %all-reduce.19.cloned.1.call-done = (f32[1,256,640]{2,1,0:T(8,128)}, f32[1,256,640]{2,1,0:T(8,128)}, f32[1,256,640]{2,1,0:T(8,128)}) async-done(((f32[1,256,640]{2,1,0:T(8,128)}, f32[1,256,640]{2,1,0:T(8,128)}, f32[1,256,640]{2,1,0:T(8,128)}), (f32[1,256,640]{2,1,0:T(8,128)}, f32[1,256,640]{2,1,0:T(8,128)}, f32[1,256,640]{2,1,0:T(8,128)})) %all-reduce.19.cloned.1.call-update) | async-done | bytes 1966096 | tf_op jit(solution)/shard_map/psum | solution.py:103
  79.1 1.3 constant_dynamic-update-slice_fusion.2
  84.2 3.0 %copy-done = f32[12,256,640]{2,1,0:T(8,128)} copy-done((f32[12,256,640]{2,1,0:T(8,128)}, f32[12,256,640]{2,1,0:T(8,128)S(1)}, u32[]{:S(2)}) %copy-start) | copy-done | bytes 7864344
  88.2 1.2 collective-permute-start
  89.8 2.1 %collective-permute-start.1 = (f32[12,256,8]{1,2,0:T(8,128)S(1)}, f32[12,256,8]{1,2,0:T(8,128)S(1)}, u32[]{:S(2)}, u32[]{:S(2)}) collective-permute-start(f32[12,256,8]{1,2,0:T(8,128)S(1)} %copy.33), channel_id=1, source_target_pairs={{1,0},{2,1},{3,2},{0,3},{5,4},{6,5},{7,6},{4,7},{9,8},{10,9},{11,1... | collective-permute-start | bytes 294920 | tf_op jit(solution)/shard_map/ppermute | solution.py:25
  91.9 1.6 %collective-permute-done = f32[12,256,8]{1,2,0:T(8,128)S(1)} collective-permute-done((f32[12,256,8]{1,2,0:T(8,128)S(1)}, f32[12,256,8]{1,2,0:T(8,128)S(1)}, u32[]{:S(2)}, u32[]{:S(2)}) %collective-permute-start) | collective-permute-done | bytes 98336 | tf_op jit(solution)/shard_map/ppermute | solution.py:23
  94.0 2.4 %collective-permute-done.1 = f32[12,256,8]{1,2,0:T(8,128)S(1)} collective-permute-done((f32[12,256,8]{1,2,0:T(8,128)S(1)}, f32[12,256,8]{1,2,0:T(8,128)S(1)}, u32[]{:S(2)}, u32[]{:S(2)}) %collective-permute-start.1) | collective-permute-done | bytes 98336 | tf_op jit(solution)/shard_map/ppermute | solution.py:25
  96.9 1.3 pad_maximum_fusion.6
  98.2 3.8 %collective-permute-start.2 = (f32[12,8,656]{2,1,0:T(8,128)S(1)}, f32[12,8,656]{2,1,0:T(8,128)S(1)}, u32[]{:S(2)}, u32[]{:S(2)}) collective-permute-start(f32[12,8,656]{2,1,0:T(8,128)S(1)} %get-tuple-element.48), channel_id=1, source_target_pairs={{0,4},{4,8},{8,12},{1,5},{5,9},{9,13},{2,6},{6,10},{10,14},{3,7},{... | collective-permute-start | bytes 755720 | tf_op jit(solution)/shard_map/ppermute | solution.py:23
  102.0 1.9 %collective-permute-start.3 = (f32[12,8,656]{2,1,0:T(8,128)S(1)}, f32[12,8,656]{2,1,0:T(8,128)S(1)}, u32[]{:S(2)}, u32[]{:S(2)}) collective-permute-start(f32[12,8,656]{2,1,0:T(8,128)S(1)} %get-tuple-element.49), channel_id=1, source_target_pairs={{4,0},{8,4},{12,8},{5,1},{9,5},{13,9},{6,2},{10,6},{14,10},{7,3},{... | collective-permute-start | bytes 755720 | tf_op jit(solution)/shard_map/ppermute | solution.py:25
  103.9 1.7 %collective-permute-done.2 = f32[12,8,656]{2,1,0:T(8,128)S(1)} collective-permute-done((f32[12,8,656]{2,1,0:T(8,128)S(1)}, f32[12,8,656]{2,1,0:T(8,128)S(1)}, u32[]{:S(2)}, u32[]{:S(2)}) %collective-permute-start.2) | collective-permute-done | bytes 251936 | tf_op jit(solution)/shard_map/ppermute | solution.py:23
  105.6 4.4 %collective-permute-done.3 = f32[12,8,656]{2,1,0:T(8,128)S(1)} collective-permute-done((f32[12,8,656]{2,1,0:T(8,128)S(1)}, f32[12,8,656]{2,1,0:T(8,128)S(1)}, u32[]{:S(2)}, u32[]{:S(2)}) %collective-permute-start.3) | collective-permute-done | bytes 251936 | tf_op jit(solution)/shard_map/ppermute | solution.py:25
  110.0 6.5 %pad_maximum_fusion = f32[12,272,656]{2,1,0:T(8,128)S(1)} fusion(f32[12,8,656]{2,1,0:T(8,128)S(1)} %collective-permute-done.3, f32[12,256,8]{2,1,0:T(8,128)S(1)} %copy.35, f32[12,256,640]{2,1,0:T(8,128)} %copy-done, f32[12,256,8]{2,1,0:T(8,128)S(1)} %copy.34, f32[12,8,656]{2,1,0:T(8,128)S(1)} %collective-permute-done.2), kind=kLoop, calls=%fused_computation.6 | loop fusion | flops 8564736 | bytes 17129472 | tf_op jit(solution)/shard_map/concatenate | solution.py:21
  116.6 1.2 subtract_multiply_fusion.7
  121.6 1.2 subtract_multiply_fusion.5
  122.8 1.6 %multiply_multiply_fusion.2 = (f32[1,272,656]{2,1,0:T(8,128)}, f32[1,272,656]{2,1,0:T(8,128)S(1)}) fusion(f32[12,272,656]{2,1,0:T(8,128)S(1)} %pad_maximum_fusion, f32[1,272,656]{2,1,0:T(8,128)S(1)} %get-tuple-element.41, f32[2,272,656]{2,1,0:T(8,128)S(1)} %get-tuple-element.68, f32[2,272,656]{2,1,0:T(8,128)S(1)} %get-tuple-element.67, ...), kind=kLoop, calls=%fused_computation.101 | loop fusion | flops 4282368 | bytes 8564736 | tf_op jit(solution)/shard_map/mul | solution.py:60
  127.5 1.2 subtract_multiply_fusion.3
  128.7 1.3 multiply_multiply_fusion.1
  130.0 1.1 add_multiply_fusion.1
  133.3 1.2 subtract_multiply_fusion.1
  135.7 1.1 slice_bitcast_fusion
  140.9 1.8 %fusion.53 = f32[256,640]{1,0:T(8,128)} fusion(f32[1,272,656]{2,1,0:T(8,128)S(1)} %get-tuple-element.24, f32[1,272,656]{2,1,0:T(8,128)S(1)} %get-tuple-element.26, f32[1,272,656]{2,1,0:T(8,128)S(1)} %copy-done.2, f32[1,272,656]{2,1,0:T(8,128)S(1)} %copy-done.1, f32[1,272,656]{2,1,0:T(8,128)S(1)} %get-tuple-element.50), kind=kLoop, calls=%fused_computation.146 | loop fusion | flops 1310720 | bytes 3932160 | tf_op jit(solution)/shard_map/squeeze | solution.py:135
  142.6 3.2 %fusion.59 = (f32[256,640]{1,0:T(8,128)}, f32[256,640]{1,0:T(8,128)}) fusion(f32[1,272,656]{2,1,0:T(8,128)S(1)} %get-tuple-element.37, f32[1,272,656]{2,1,0:T(8,128)S(1)} %get-tuple-element.59, f32[1,272,656]{2,1,0:T(8,128)S(1)} %get-tuple-element.57, f32[1,272,656]{2,1,0:T(8,128)S(1)} %get-tuple-element.34, f32[1,272,656]{2,1,0:T(8,128)S(1)} %get-tuple-element.43, ...), kind=kLoop, calls=%fused_computation.155 | loop fusion | flops 2621440 | bytes 9175040 | tf_op jit(solution)/shard_map/squeeze | solution.py:135
  (81 shorter events, 20.3 us)
Async XLA Ops:
  7.2 71.9 %all-reduce.19.cloned.1.call-start = ((), (), s32[]{:S(2)}) async-start(), calls=%async_computation | async-start | bytes 3932160 | tf_op jit(solution)/shard_map/psum | solution.py:103
  79.1 1.3 copy-start.13
  79.1 1.5 copy-start.12
  79.1 1.7 %copy-start.3 = (f32[256,640]{1,0:T(8,128)S(1)}, f32[256,640]{1,0:T(8,128)}, u32[]{:S(2)}) copy-start(f32[256,640]{1,0:T(8,128)} %param.25) | copy-start | bytes 1966084
  80.4 1.2 copy-start.4
  80.6 1.2 copy-start.5
  80.8 1.2 copy-start.6
  81.6 1.2 copy-start.7
  81.7 1.2 copy-start.8
  81.9 1.2 copy-start.9
  82.7 1.2 copy-start.10
  82.9 1.2 copy-start.11
  84.1 3.1 %copy-start = (f32[12,256,640]{2,1,0:T(8,128)}, f32[12,256,640]{2,1,0:T(8,128)S(1)}, u32[]{:S(2)}) copy-start(f32[12,256,640]{2,1,0:T(8,128)S(1)} %bitcast_dynamic-update-slice_fusion) | copy-start | bytes 23592964
  88.2 5.4 %collective-permute-start = (f32[12,256,8]{1,2,0:T(8,128)S(1)}, f32[12,256,8]{1,2,0:T(8,128)S(1)}, u32[]{:S(2)}, u32[]{:S(2)}) collective-permute-start(f32[12,256,8]{1,2,0:T(8,128)S(1)} %copy.32), channel_id=1, source_target_pairs={{0,1},{1,2},{2,3},{3,0},{4,5},{5,6},{6,7},{7,4},{8,9},{9,10},{10,1... | collective-permute-start | bytes 294920 | tf_op jit(solution)/shard_map/ppermute | solution.py:23
  89.8 6.6 %collective-permute-start.1 = (f32[12,256,8]{1,2,0:T(8,128)S(1)}, f32[12,256,8]{1,2,0:T(8,128)S(1)}, u32[]{:S(2)}, u32[]{:S(2)}) collective-permute-start(f32[12,256,8]{1,2,0:T(8,128)S(1)} %copy.33), channel_id=1, source_target_pairs={{1,0},{2,1},{3,2},{0,3},{5,4},{6,5},{7,6},{4,7},{9,8},{10,9},{11,1... | collective-permute-start | bytes 294920 | tf_op jit(solution)/shard_map/ppermute | solution.py:25
  98.2 7.4 %collective-permute-start.2 = (f32[12,8,656]{2,1,0:T(8,128)S(1)}, f32[12,8,656]{2,1,0:T(8,128)S(1)}, u32[]{:S(2)}, u32[]{:S(2)}) collective-permute-start(f32[12,8,656]{2,1,0:T(8,128)S(1)} %get-tuple-element.48), channel_id=1, source_target_pairs={{0,4},{4,8},{8,12},{1,5},{5,9},{9,13},{2,6},{6,10},{10,14},{3,7},{... | collective-permute-start | bytes 755720 | tf_op jit(solution)/shard_map/ppermute | solution.py:23
  102.0 8.0 %collective-permute-start.3 = (f32[12,8,656]{2,1,0:T(8,128)S(1)}, f32[12,8,656]{2,1,0:T(8,128)S(1)}, u32[]{:S(2)}, u32[]{:S(2)}) collective-permute-start(f32[12,8,656]{2,1,0:T(8,128)S(1)} %get-tuple-element.49), channel_id=1, source_target_pairs={{4,0},{8,4},{12,8},{5,1},{9,5},{13,9},{6,2},{10,6},{14,10},{7,3},{... | collective-permute-start | bytes 755720 | tf_op jit(solution)/shard_map/ppermute | solution.py:25
  139.4 1.2 copy-start.1
  139.5 1.4 copy-start.2
Sparse Core Ops, SparseCore 0:
  17.0 62.0 all-reduce.18
where the time goes:
time: 153 us
  waiting for transfers between devices  72.3 us (47%)
  other arithmetic  42.8 us (28%)
  between operations  14.4 us (9%)
  local copies, waits for them, and re-layouts  14.1 us (9%)
  starting transfers between devices  9.05 us (6%)
    psum x1, waiting for transfers between devices, shards(): lax.psum((jnp.sum(weighted, axis=0), jnp.sum(cover * height, axis=0), jnp...  62.2 us
    reduce_sum x1, other arithmetic, shards(): jnp.sum(cover * height, axis=0)  9.63 us
    unnamed x38, local copies, waits for them, and re-layouts  9.22 us
    mul x8, other arithmetic, slopes(): 0.5 * (along[:, :, 2:] - along[:, :, :-2])  6.78 us
    ppermute x2, waiting for transfers between devices, extended(): lax.ppermute(head, axis, [((i + 1) % count, i) for i in range(ends)])  6.75 us
    concatenate x1, other arithmetic, extended(): jnp.concatenate([lax.ppermute(tail, axis, [(i, (i + 1) % count) for i in...  6.47 us
    ppermute x2, starting transfers between devices, extended(): lax.ppermute(tail, axis, [(i, (i + 1) % count) for i in range(ends)])  5.01 us
    squeeze x2, other arithmetic, shards(): return (velocity[0], velocity[1], stresses[0], stresses[1], stresses[2])  4.95 us
  transfers between devices with their start and end apart: 5, of which 5 were waited for; matrix products, arithmetic and copies ran while one was open for 1% of the time, Pallas kernels for 0%

commit v1 on v0

--- a/solution.py
+++ b/solution.py
@@ -100,9 +100,16 @@
     height = thickness.astype(jnp.float32)
     cover = area.astype(jnp.float32) * present
     weighted = ridge_weight[:, None, None] * cover * height * height
-    strength, mass, concentration = lax.psum(
-        (jnp.sum(weighted, axis=0), jnp.sum(cover * height, axis=0), jnp.sum(cover, axis=0)), "cat"
+    partial = jnp.stack(
+        [jnp.sum(weighted, axis=0), jnp.sum(cover * height, axis=0), jnp.sum(cover, axis=0)]
     )
+    count = lax.axis_size("cat")
+    totals = partial
+    for shift in range(1, count):
+        totals = totals + lax.ppermute(
+            partial, "cat", [(i, (i + shift) % count) for i in range(count)]
+        )
+    strength, mass, concentration = totals
     wet = land_mask.astype(jnp.float32)
     margin = 2 * SUB
     bundle = jnp.stack(

time: 153 us -> 120 us (0.78)
  waiting for transfers between devices: 72.3 us -> 51.8 us
  between operations: 14.4 us -> 1.08 us
  starting transfers between devices: 9.05 us -> 12.5 us
    psum x1 -> x0, waiting for transfers between devices: 62.2 us -> none  [shards(): lax.psum((jnp.sum(weighted, axis=0), jnp.sum(cover * height, axis=0), jnp...]
    ppermute x0 -> x1, waiting for transfers between devices: none -> 42.5 us  [shards(): lax.ppermute(partial, 'cat', [(i, (i + shift) % count) for i in range(cou...]
    ppermute x0 -> x1, starting transfers between devices: none -> 2.09 us  [shards(): lax.ppermute(partial, 'cat', [(i, (i + shift) % count) for i in range(cou...]
    unnamed x38 -> x31, local copies, waits for them, and re-layouts: 9.22 us -> 7.87 us
where the time goes in v1:
time: 120 us
  waiting for transfers between devices  51.8 us (43%)
  other arithmetic  42 us (35%)
  local copies, waits for them, and re-layouts  12.7 us (11%)
  starting transfers between devices  12.5 us (10%)
    ppermute x1, waiting for transfers between devices, shards(): lax.ppermute(partial, 'cat', [(i, (i + shift) % count) for i in range(cou...  42.5 us
    reduce_sum x1, other arithmetic, shards(): jnp.sum(weighted, axis=0)  8.56 us
    unnamed x31, local copies, waits for them, and re-layouts  7.87 us
    mul x8, other arithmetic, slopes(): 0.5 * (along[:, :, 2:] - along[:, :, :-2])  6.78 us
    concatenate x1, other arithmetic, extended(): jnp.concatenate([lax.ppermute(tail, axis, [(i, (i + 1) % count) for i in...  6.47 us
    ppermute x2, starting transfers between devices, extended(): lax.ppermute(tail, axis, [(i, (i + 1) % count) for i in range(ends)])  6.41 us
    ppermute x2, waiting for transfers between devices, extended(): lax.ppermute(head, axis, [((i + 1) % count, i) for i in range(ends)])  5.88 us
    squeeze x2, other arithmetic, shards(): return (velocity[0], velocity[1], stresses[0], stresses[1], stresses[2])  4.95 us
  transfers between devices with their start and end apart: 5, of which 5 were waited for; matrix products, arithmetic and copies ran while one was open for 1% of the time, Pallas kernels for 0%

profile of v1, /device:TPU:1, one launch (start us, length us, event | category | flops | bytes accessed | tf_op | source)
XLA Modules:
  0.0 120.1 jit_solution(6025799139851370533)
XLA Ops:
  0.6 8.6 %fusion.1 = (f32[256,640]{1,0:T(8,128)S(1)}, f32[256,640]{1,0:T(8,128)S(1)}, f32[256,640]{1,0:T(8,128)S(1)}) fusion(bf16[20,256,640]{2,1,0:T(8,128)(2,1)} %param.13, bf16[20,256,640]{2,1,0:T(8,128)(2,1)} %param.14, s32[256,640]{1,0:T(8,128)} %param.16, f32[20]{0:T(128)} %param.15, s32[20]{0:T(128)S(1)} %iota_add_fusion), kind=kLoop, calls=%fused_computation.3 | loop fusion | flops 35553280 | bytes 15728800 | tf_op jit(solution)/shard_map/reduce_sum | solution.py:104
  9.4 2.1 %collective-permute-start = (f32[3,256,640]{2,1,0:T(8,128)S(1)}, f32[3,256,640]{2,1,0:T(8,128)S(1)}, u32[]{:S(2)}, u32[]{:S(2)}) collective-permute-start(f32[3,256,640]{2,1,0:T(8,128)S(1)} %pad_maximum_fusion.1), channel_id=1, source_target_pairs={{0,16},{16,0},{1,17},{17,1},{2,18},{18,2},{3,19},{19,3},{4,20},{20... | collective-permute-start | bytes 5898248 | tf_op jit(solution)/shard_map/ppermute | solution.py:109
  11.5 42.5 %collective-permute-done = f32[3,256,640]{2,1,0:T(8,128)S(1)} collective-permute-done((f32[3,256,640]{2,1,0:T(8,128)S(1)}, f32[3,256,640]{2,1,0:T(8,128)S(1)}, u32[]{:S(2)}, u32[]{:S(2)}) %collective-permute-start) | collective-permute-done | bytes 1966112 | tf_op jit(solution)/shard_map/ppermute | solution.py:109
  57.9 3.1 %copy-done = f32[12,256,640]{2,1,0:T(8,128)} copy-done((f32[12,256,640]{2,1,0:T(8,128)}, f32[12,256,640]{2,1,0:T(8,128)S(1)}, u32[]{:S(2)}) %copy-start) | copy-done | bytes 7864344
  61.9 1.3 %collective-permute-start.1 = (f32[12,256,8]{1,2,0:T(8,128)S(1)}, f32[12,256,8]{1,2,0:T(8,128)S(1)}, u32[]{:S(2)}, u32[]{:S(2)}) collective-permute-start(f32[12,256,8]{1,2,0:T(8,128)S(1)} %copy.32), channel_id=1, source_target_pairs={{0,1},{1,2},{2,3},{3,0},{4,5},{5,6},{6,7},{7,4},{8,9},{9,10},{10,1... | collective-permute-start | bytes 294920 | tf_op jit(solution)/shard_map/ppermute | solution.py:23
  63.6 2.1 %collective-permute-start.2 = (f32[12,256,8]{1,2,0:T(8,128)S(1)}, f32[12,256,8]{1,2,0:T(8,128)S(1)}, u32[]{:S(2)}, u32[]{:S(2)}) collective-permute-start(f32[12,256,8]{1,2,0:T(8,128)S(1)} %copy.33), channel_id=1, source_target_pairs={{1,0},{2,1},{3,2},{0,3},{5,4},{6,5},{7,6},{4,7},{9,8},{10,9},{11,1... | collective-permute-start | bytes 294920 | tf_op jit(solution)/shard_map/ppermute | solution.py:25
  65.7 1.6 %collective-permute-done.1 = f32[12,256,8]{1,2,0:T(8,128)S(1)} collective-permute-done((f32[12,256,8]{1,2,0:T(8,128)S(1)}, f32[12,256,8]{1,2,0:T(8,128)S(1)}, u32[]{:S(2)}, u32[]{:S(2)}) %collective-permute-start.1) | collective-permute-done | bytes 98336 | tf_op jit(solution)/shard_map/ppermute | solution.py:23
  67.8 1.5 %collective-permute-done.2 = f32[12,256,8]{1,2,0:T(8,128)S(1)} collective-permute-done((f32[12,256,8]{1,2,0:T(8,128)S(1)}, f32[12,256,8]{1,2,0:T(8,128)S(1)}, u32[]{:S(2)}, u32[]{:S(2)}) %collective-permute-start.2) | collective-permute-done | bytes 98336 | tf_op jit(solution)/shard_map/ppermute | solution.py:25
  69.8 1.3 %pad_maximum_fusion.7 = (f32[12,8,656]{2,1,0:T(8,128)S(1)}, f32[12,8,656]{2,1,0:T(8,128)S(1)}) fusion(f32[12,256,8]{2,1,0:T(8,128)S(1)} %copy.35, f32[12,256,640]{2,1,0:T(8,128)} %copy-done, f32[12,256,8]{2,1,0:T(8,128)S(1)} %copy.34), kind=kLoop, calls=%fused_computation.179 | loop fusion | flops 251904 | bytes 8564736 | tf_op jit(solution)/shard_map/slice | solution.py:20
  71.1 5.1 %collective-permute-start.3 = (f32[12,8,656]{2,1,0:T(8,128)S(1)}, f32[12,8,656]{2,1,0:T(8,128)S(1)}, u32[]{:S(2)}, u32[]{:S(2)}) collective-permute-start(f32[12,8,656]{2,1,0:T(8,128)S(1)} %get-tuple-element.45), channel_id=1, source_target_pairs={{0,4},{4,8},{8,12},{1,5},{5,9},{9,13},{2,6},{6,10},{10,14},{3,7},{... | collective-permute-start | bytes 755720 | tf_op jit(solution)/shard_map/ppermute | solution.py:23
  76.2 1.9 %collective-permute-start.4 = (f32[12,8,656]{2,1,0:T(8,128)S(1)}, f32[12,8,656]{2,1,0:T(8,128)S(1)}, u32[]{:S(2)}, u32[]{:S(2)}) collective-permute-start(f32[12,8,656]{2,1,0:T(8,128)S(1)} %get-tuple-element.46), channel_id=1, source_target_pairs={{4,0},{8,4},{12,8},{5,1},{9,5},{13,9},{6,2},{10,6},{14,10},{7,3},{... | collective-permute-start | bytes 755720 | tf_op jit(solution)/shard_map/ppermute | solution.py:25
  78.1 1.7 %collective-permute-done.3 = f32[12,8,656]{2,1,0:T(8,128)S(1)} collective-permute-done((f32[12,8,656]{2,1,0:T(8,128)S(1)}, f32[12,8,656]{2,1,0:T(8,128)S(1)}, u32[]{:S(2)}, u32[]{:S(2)}) %collective-permute-start.3) | collective-permute-done | bytes 251936 | tf_op jit(solution)/shard_map/ppermute | solution.py:23
  79.8 4.4 %collective-permute-done.4 = f32[12,8,656]{2,1,0:T(8,128)S(1)} collective-permute-done((f32[12,8,656]{2,1,0:T(8,128)S(1)}, f32[12,8,656]{2,1,0:T(8,128)S(1)}, u32[]{:S(2)}, u32[]{:S(2)}) %collective-permute-start.4) | collective-permute-done | bytes 251936 | tf_op jit(solution)/shard_map/ppermute | solution.py:25
  84.2 6.5 %pad_maximum_fusion = f32[12,272,656]{2,1,0:T(8,128)S(1)} fusion(f32[12,8,656]{2,1,0:T(8,128)S(1)} %collective-permute-done.4, f32[12,256,8]{2,1,0:T(8,128)S(1)} %copy.35, f32[12,256,640]{2,1,0:T(8,128)} %copy-done, f32[12,256,8]{2,1,0:T(8,128)S(1)} %copy.34, f32[12,8,656]{2,1,0:T(8,128)S(1)} %collective-permute-done.3), kind=kLoop, calls=%fused_computation.6 | loop fusion | flops 8564736 | bytes 17129472 | tf_op jit(solution)/shard_map/concatenate | solution.py:21
  90.8 1.2 subtract_multiply_fusion.7
  95.8 1.2 subtract_multiply_fusion.5
  97.0 1.6 %multiply_multiply_fusion.2 = (f32[1,272,656]{2,1,0:T(8,128)}, f32[1,272,656]{2,1,0:T(8,128)S(1)}) fusion(f32[12,272,656]{2,1,0:T(8,128)S(1)} %pad_maximum_fusion, f32[1,272,656]{2,1,0:T(8,128)S(1)} %get-tuple-element.38, f32[2,272,656]{2,1,0:T(8,128)S(1)} %get-tuple-element.65, f32[2,272,656]{2,1,0:T(8,128)S(1)} %get-tuple-element.64, ...), kind=kLoop, calls=%fused_computation.103 | loop fusion | flops 4282368 | bytes 8564736 | tf_op jit(solution)/shard_map/mul | solution.py:60
  101.7 1.2 subtract_multiply_fusion.3
  102.9 1.3 %multiply_multiply_fusion.1 = (f32[1,272,656]{2,1,0:T(8,128)}, f32[1,272,656]{2,1,0:T(8,128)S(1)}) fusion(f32[2,272,656]{2,1,0:T(8,128)S(1)} %get-tuple-element.61, f32[2,272,656]{2,1,0:T(8,128)S(1)} %get-tuple-element.60, f32[12,272,656]{2,1,0:T(8,128)S(1)} %pad_maximum_fusion), kind=kLoop, calls=%fused_computation.102 | loop fusion | flops 2498048 | bytes 4996096 | tf_op jit(solution)/shard_map/div | solution.py:60
  104.3 1.1 add_multiply_fusion.1
  107.6 1.2 subtract_multiply_fusion.1
  110.0 1.1 slice_bitcast_fusion
  115.1 1.8 %fusion.53 = f32[256,640]{1,0:T(8,128)} fusion(f32[1,272,656]{2,1,0:T(8,128)S(1)} %get-tuple-element.21, f32[1,272,656]{2,1,0:T(8,128)S(1)} %get-tuple-element.23, f32[1,272,656]{2,1,0:T(8,128)S(1)} %copy-done.2, f32[1,272,656]{2,1,0:T(8,128)S(1)} %copy-done.1, f32[1,272,656]{2,1,0:T(8,128)S(1)} %get-tuple-element.47), kind=kLoop, calls=%fused_computation.148 | loop fusion | flops 1310720 | bytes 3932160 | tf_op jit(solution)/shard_map/squeeze | solution.py:142
  116.9 3.2 %fusion.59 = (f32[256,640]{1,0:T(8,128)}, f32[256,640]{1,0:T(8,128)}) fusion(f32[1,272,656]{2,1,0:T(8,128)S(1)} %get-tuple-element.34, f32[1,272,656]{2,1,0:T(8,128)S(1)} %get-tuple-element.56, f32[1,272,656]{2,1,0:T(8,128)S(1)} %get-tuple-element.54, f32[1,272,656]{2,1,0:T(8,128)S(1)} %get-tuple-element.31, f32[1,272,656]{2,1,0:T(8,128)S(1)} %get-tuple-element.40, ...), kind=kLoop, calls=%fused_computation.157 | loop fusion | flops 2621440 | bytes 9175040 | tf_op jit(solution)/shard_map/squeeze | solution.py:142
  (75 shorter events, 20.4 us)
Async XLA Ops:
  9.3 44.8 %copy-start.3 = (f32[256,640]{1,0:T(8,128)S(1)}, f32[256,640]{1,0:T(8,128)}, u32[]{:S(2)}) copy-start(f32[256,640]{1,0:T(8,128)} %param.25) | copy-start | bytes 1966084
  9.4 44.6 %collective-permute-start = (f32[3,256,640]{2,1,0:T(8,128)S(1)}, f32[3,256,640]{2,1,0:T(8,128)S(1)}, u32[]{:S(2)}, u32[]{:S(2)}) collective-permute-start(f32[3,256,640]{2,1,0:T(8,128)S(1)} %pad_maximum_fusion.1), channel_id=1, source_target_pairs={{0,16},{16,0},{1,17},{17,1},{2,18},{18,2},{3,19},{19,3},{4,20},{20... | collective-permute-start | bytes 5898248 | tf_op jit(solution)/shard_map/ppermute | solution.py:109
  54.2 1.1 copy-start.4
  54.2 1.3 %copy-start.5 = (f32[256,640]{1,0:T(8,128)S(1)}, f32[256,640]{1,0:T(8,128)}, u32[]{:S(2)}) copy-start(f32[256,640]{1,0:T(8,128)} %param.24) | copy-start | bytes 1966084
  54.2 1.5 %copy-start.6 = (s32[256,640]{1,0:T(8,128)S(1)}, s32[256,640]{1,0:T(8,128)}, u32[]{:S(2)}) copy-start(s32[256,640]{1,0:T(8,128)} %param.17) | copy-start | bytes 1966084
  55.3 1.2 copy-start.7
  55.5 1.2 copy-start.8
  55.7 1.2 copy-start.9
  56.5 1.2 copy-start.10
  56.6 1.2 copy-start.11
  57.9 3.1 %copy-start = (f32[12,256,640]{2,1,0:T(8,128)}, f32[12,256,640]{2,1,0:T(8,128)S(1)}, u32[]{:S(2)}) copy-start(f32[12,256,640]{2,1,0:T(8,128)S(1)} %bitcast_dynamic-update-slice_fusion) | copy-start | bytes 23592964
  61.9 5.4 %collective-permute-start.1 = (f32[12,256,8]{1,2,0:T(8,128)S(1)}, f32[12,256,8]{1,2,0:T(8,128)S(1)}, u32[]{:S(2)}, u32[]{:S(2)}) collective-permute-start(f32[12,256,8]{1,2,0:T(8,128)S(1)} %copy.32), channel_id=1, source_target_pairs={{0,1},{1,2},{2,3},{3,0},{4,5},{5,6},{6,7},{7,4},{8,9},{9,10},{10,1... | collective-permute-start | bytes 294920 | tf_op jit(solution)/shard_map/ppermute | solution.py:23
  63.6 5.7 %collective-permute-start.2 = (f32[12,256,8]{1,2,0:T(8,128)S(1)}, f32[12,256,8]{1,2,0:T(8,128)S(1)}, u32[]{:S(2)}, u32[]{:S(2)}) collective-permute-start(f32[12,256,8]{1,2,0:T(8,128)S(1)} %copy.33), channel_id=1, source_target_pairs={{1,0},{2,1},{3,2},{0,3},{5,4},{6,5},{7,6},{4,7},{9,8},{10,9},{11,1... | collective-permute-start | bytes 294920 | tf_op jit(solution)/shard_map/ppermute | solution.py:25
  71.1 8.8 %collective-permute-start.3 = (f32[12,8,656]{2,1,0:T(8,128)S(1)}, f32[12,8,656]{2,1,0:T(8,128)S(1)}, u32[]{:S(2)}, u32[]{:S(2)}) collective-permute-start(f32[12,8,656]{2,1,0:T(8,128)S(1)} %get-tuple-element.45), channel_id=1, source_target_pairs={{0,4},{4,8},{8,12},{1,5},{5,9},{9,13},{2,6},{6,10},{10,14},{3,7},{... | collective-permute-start | bytes 755720 | tf_op jit(solution)/shard_map/ppermute | solution.py:23
  76.2 8.0 %collective-permute-start.4 = (f32[12,8,656]{2,1,0:T(8,128)S(1)}, f32[12,8,656]{2,1,0:T(8,128)S(1)}, u32[]{:S(2)}, u32[]{:S(2)}) collective-permute-start(f32[12,8,656]{2,1,0:T(8,128)S(1)} %get-tuple-element.46), channel_id=1, source_target_pairs={{4,0},{8,4},{12,8},{5,1},{9,5},{13,9},{6,2},{10,6},{14,10},{7,3},{... | collective-permute-start | bytes 755720 | tf_op jit(solution)/shard_map/ppermute | solution.py:25
  113.7 1.2 copy-start.1
  113.7 1.4 %copy-start.2 = (f32[1,272,656]{2,1,0:T(8,128)S(1)}, f32[1,272,656]{2,1,0:T(8,128)}, u32[]{:S(2)}) copy-start(f32[1,272,656]{2,1,0:T(8,128)} %get-tuple-element.15) | copy-start | bytes 2141188
